TPU v7x, 256 devices: a whole 4x4x8 slice. The times are simulated.
256 devices in a mesh: store: 16 (over x, y_hi, core), tp: 16 (over y_lo, z).
Axes of the slice: x: 4, y: 4 (y_hi: 2, y_lo: 2; y = y_hi * 2 + y_lo), z: 8, core: 2. Of those that a mesh axis runs over, the one named last changes fastest.
Arguments:
- hidden: bfloat16 [16, 576, 8192], P('store', None, 'tp'), may hold values from -300 to 300
- w_query: bfloat16 [8192, 4096], P(None, 'tp'), may hold values from -0.0625 to 0.0625
- w_keyvalue: bfloat16 [8192, 1024], P('tp'), may hold values from -0.1875 to 0.1875
- passage_cache: bfloat16 [64, 4, 384, 256], P('store'), may hold values from -400 to 400
- passage_ids: int32 [16, 8], replicated, may hold values from 0 to 63, as said below
- select_index: int32 [16, 576], P('store'), may hold values from 0 to 3071, as said below
- select_count: int32 [16], P('store'), may hold values from 288 to 576, as said below
Outputs:
- context: bfloat16 [16, 576, 4096], P('store', None, 'tp')
Inputs may be any that keep to these rules, and one draw needn't show every extreme that they name: `passage_ids`: the passages of one prompt lie in distinct shards of the pool, shard = id // 4. `select_index`: all entries of a row are distinct positions of the prompt; the first select_count[p] of row p are in increasing order, the others are ignored. `select_count`: some prompt of every draw has 576 selected tokens.
All inputs are finite; a program needn't handle non-finite values.
Results may differ from a plain program's by a relative error of at most 0.04.
Values may be sent and summed in bfloat16 or wider, within the bound.
A program may use at most 128 MiB of HBM per device.

v0:
```python
import jax
import jax.numpy as jnp
from jax import lax
from jax.sharding import Mesh
from jax.sharding import PartitionSpec as P

D = 8192
KV_HEADS = 4
HEAD_DIM = 128
PASSAGE = 384
PASSAGES = 8
SEQ = 3072
TP = ("tp_0", "tp_1")
ROPE_BASE = 1000000.0
EPSILON = 1e-06


def in_blocks(value, dim, length):
    shape = value.shape
    parts = value.reshape(*shape[:dim], length, shape[dim] // length, *shape[dim + 1 :])
    return jnp.moveaxis(parts, dim, 0)


def summed_on_arrival(value, axis, dim):
    parts = in_blocks(value, dim, lax.axis_size(axis))
    arrived = lax.all_to_all(parts, axis, split_axis=0, concat_axis=0, tiled=True)
    return arrived.astype(jnp.float32).sum(axis=0)


def from_partner(value, axis, bit):
    return lax.ppermute(value, axis, [(i, i ^ 1 << bit) for i in range(lax.axis_size(axis))])


def joined_along(parts, dim):
    shape = list(parts.shape[1:])
    shape[dim] *= parts.shape[0]
    return jnp.moveaxis(parts, 0, dim).reshape(shape)


def stacked_from(value, axes, sequence):
    parts = value[None]
    for k in sequence:
        parts = lax.all_gather(parts, axes[k], axis=0, tiled=True)
    held = [lax.axis_size(axes[k]) for k in reversed(sequence)]
    parts = parts.reshape(*held, *value.shape)
    turned = sorted(range(len(sequence)), key=lambda place: sequence[len(sequence) - 1 - place])
    return parts.transpose(*turned, *range(len(sequence), parts.ndim)).reshape(-1, *value.shape)


def gather_axes(value, axes, sequence, dim):
    return joined_along(stacked_from(value, axes, sequence), dim)


def rotate(vectors, positions):
    half_dim = vectors.shape[-1] // 2
    frequency = ROPE_BASE ** (-(jnp.arange(half_dim, dtype=jnp.float32) * 2.0) / vectors.shape[-1])
    angles = positions.astype(jnp.float32)[..., None] * frequency
    cosine = jnp.cos(angles)
    sine_part = jnp.sin(angles)
    front_half = vectors[..., :half_dim]
    back_half = vectors[..., half_dim:]
    return jnp.concatenate(
        [front_half * cosine - back_half * sine_part, back_half * cosine + front_half * sine_part],
        axis=-1,
    )


def local(hidden, w_query, w_keyvalue, passage_cache, passage_ids, select_index, select_count):
    tp_count = lax.axis_size(TP)
    group_width = tp_count // KV_HEADS
    tp_rank = lax.axis_index(TP)
    kv_head = tp_rank // group_width
    store_rank = lax.axis_index("store")
    local_heads = w_query.shape[1] // HEAD_DIM
    row_count = hidden.shape[1]
    pool_dev = passage_cache.shape[0]
    partial_kv = jnp.dot(hidden[0], w_keyvalue, preferred_element_type=jnp.float32)
    head_kv = summed_on_arrival(partial_kv.astype(jnp.bfloat16), TP, 1)
    levels = group_width.bit_length() - 1
    for level in range(levels):
        partner = from_partner(head_kv.astype(jnp.bfloat16), TP, level).astype(head_kv.dtype)
        upper = tp_rank // 2**level % 2 == 1
        head_kv = jnp.where(
            upper,
            jnp.concatenate([partner, head_kv], axis=1),
            jnp.concatenate([head_kv, partner], axis=1),
        )
    token_part = gather_axes(hidden, TP, (0, 1), 2)[0]
    widened = token_part.astype(jnp.float32)
    running = jnp.dot(token_part, w_query, preferred_element_type=jnp.float32)
    squares = jnp.sum(widened * widened, axis=-1)
    inverse_rms = lax.rsqrt(squares / D + EPSILON)
    positions = select_index[0]
    live_count = select_count[0]
    queries = rotate(
        (running * inverse_rms[:, None]).reshape(row_count, local_heads, HEAD_DIM),
        positions[:, None],
    )
    queries = (queries * HEAD_DIM ** (-0.5)).astype(jnp.bfloat16)
    key_value = head_kv * inverse_rms[:, None]
    new_keys = rotate(key_value[:, :HEAD_DIM], positions).astype(jnp.bfloat16)
    new_values = key_value[:, HEAD_DIM:].astype(jnp.bfloat16)
    head_cache = lax.dynamic_index_in_dim(passage_cache, kv_head, 1, keepdims=False)
    owners = passage_ids // pool_dev
    local_index = passage_ids % pool_dev
    matches = owners == store_rank
    local_slot = jnp.sum(jnp.where(matches, local_index, 0), axis=1)
    present = jnp.any(matches, axis=1)
    outgoing = jnp.take(head_cache, local_slot, axis=0) * present[:, None, None].astype(
        jnp.bfloat16
    )
    incoming = lax.all_to_all(outgoing, "store", split_axis=0, concat_axis=0, tiled=True)
    my_owners = lax.dynamic_index_in_dim(owners, store_rank, 0, keepdims=False)
    fetched = jnp.take(incoming, my_owners, axis=0)
    offsets = jnp.arange(PASSAGES) * PASSAGE
    old_keys = rotate(fetched[..., :HEAD_DIM].astype(jnp.float32), offsets[:, None]).astype(
        jnp.bfloat16
    )
    old_keys = old_keys.reshape(SEQ, HEAD_DIM)
    old_values = fetched[..., HEAD_DIM:].reshape(SEQ, HEAD_DIM)
    row_ids = jnp.arange(row_count, dtype=jnp.int32)
    target = jnp.where(row_ids < live_count, positions, SEQ)
    all_keys = old_keys.at[target].set(new_keys, mode="drop")
    all_values = old_values.at[target].set(new_values, mode="drop")
    allowed = jnp.arange(SEQ, dtype=jnp.int32)[None, :] <= positions[:, None]
    scores = jnp.einsum("rgd,sd->grs", queries, all_keys, preferred_element_type=jnp.float32)
    scores = jnp.where(allowed[None], scores, -jnp.inf)
    row_max = jnp.max(scores, axis=-1, keepdims=True)
    shifted = jnp.exp(scores - row_max)
    weight = (shifted / jnp.sum(shifted, axis=-1, keepdims=True)).astype(jnp.bfloat16)
    context = jnp.einsum("grs,sd->rgd", weight, all_values, preferred_element_type=jnp.float32)
    row_live = (row_ids < live_count)[:, None, None]
    context = jnp.where(row_live, context, 0.0)
    return context.reshape(1, row_count, local_heads * HEAD_DIM).astype(jnp.bfloat16)


def solution(mesh):
    split = Mesh(mesh.devices.reshape(mesh.shape["store"], 2, 8), ("store", "tp_0", "tp_1"))
    placed = (
        P("store", None, TP),
        P(None, TP),
        P(TP, None),
        P("store", None, None, None),
        P(),
        P("store", None),
        P("store"),
    )
    return jax.shard_map(
        local, mesh=split, in_specs=placed, out_specs=P("store", None, TP), check_vma=False
    )
```

profile of v0, /device:TPU:33, one launch (start us, length us, event | category | flops | bytes accessed | tf_op | source)
XLA Modules:
  0.0 259.8 jit_solution(8467378492987644100)
XLA Ops:
  7.3 32.1 %all-gather.5.cloned.1.call-done = bf16[2,576,512]{2,1,0:T(8,128)(2,1)} async-done(((bf16[1,576,512]{2,1,0:T(8,128)(2,1)}), bf16[2,576,512]{2,1,0:T(8,128)(2,1)}) %all-gather.5.cloned.1.call-update) | async-done | bytes 1179664 | tf_op jit(solution)/shard_map/all_gather | solution.py:43
  39.5 3.2 %convolution_convert_fusion = bf16[576,1024]{1,0:T(8,128)(2,1)} fusion(bf16[512,1024]{1,0:T(8,128)(2,1)} %param.9, bf16[1,576,512]{2,1,0:T(8,128)(2,1)} %param.7), kind=kOutput, calls=%fused_computation.19 | convolution fusion | flops 604569600 | bytes 2818048 | tf_op jit(solution)/shard_map/dot_general | solution.py:77
  42.7 2.4 copy.39
  45.1 6.9 %all-to-all-start.1 = ((bf16[16,576,64]{1,2,0:T(8,128)(2,1)}), bf16[16,576,64]{1,2,0:T(8,128)(2,1)}, u32[]{:S(2)}, u32[]{:S(2)}) async-start(bf16[16,576,64]{1,2,0:T(8,128)(2,1)} %bitcast.72), calls=%async_computation.1 | async-start | bytes 2621440 | tf_op jit(solution)/shard_map/all_to_all | solution.py:26
  53.1 1.9 gather_fusion
  55.0 2.0 select_multiply_fusion
  57.0 33.9 %all-to-all-done.1 = bf16[16,576,64]{1,2,0:T(8,128)(2,1)} async-done(((bf16[16,576,64]{1,2,0:T(8,128)(2,1)}), bf16[16,576,64]{1,2,0:T(8,128)(2,1)}, u32[]{:S(2)}, u32[]{:S(2)}) %all-to-all-start.1) | async-done | bytes 1179680 | tf_op jit(solution)/shard_map/all_to_all | solution.py:26
  90.9 12.1 %all-to-all-start = ((bf16[16,384,256]{2,1,0:T(8,128)(2,1)}), bf16[16,384,256]{2,1,0:T(8,128)(2,1)S(1)}, u32[]{:S(2)}, u32[]{:S(2)}) async-start(bf16[16,384,256]{2,1,0:T(8,128)(2,1)} %select_multiply_fusion), calls=%async_computation | async-start | bytes 6291456 | tf_op jit(solution)/shard_map/all_to_all | solution.py:112
  104.0 2.6 iota_compare_fusion
  106.6 1.5 convert_reduce_fusion
  108.2 4.4 %collective-permute-start = (bf16[576,64]{0,1:T(8,128)(2,1)S(1)}, bf16[576,64]{0,1:T(8,128)(2,1)S(1)}, u32[]{:S(2)}, u32[]{:S(2)}) collective-permute-start(bf16[576,64]{0,1:T(8,128)(2,1)S(1)} %convert_element_type.92), channel_id=1, source_target_pairs={{0,1},{1,0},{2,3},{3,2},{4,5},{5,4},{6,7},{7,6},{8,9},{9,8},{10,11... | collective-permute-start | bytes 221192 | tf_op jit(solution)/shard_map/ppermute | solution.py:31
  112.5 4.9 %collective-permute-done = bf16[576,64]{0,1:T(8,128)(2,1)S(1)} collective-permute-done((bf16[576,64]{0,1:T(8,128)(2,1)S(1)}, bf16[576,64]{0,1:T(8,128)(2,1)S(1)}, u32[]{:S(2)}, u32[]{:S(2)}) %collective-permute-start) | collective-permute-done | bytes 73760 | tf_op jit(solution)/shard_map/ppermute | solution.py:31
  118.3 11.2 %collective-permute-done.1 = bf16[576,128]{0,1:T(8,128)(2,1)} collective-permute-done((bf16[576,128]{0,1:T(8,128)(2,1)}, bf16[576,128]{0,1:T(8,128)(2,1)}, u32[]{:S(2)}, u32[]{:S(2)}) %collective-permute-start.1) | collective-permute-done | bytes 147488 | tf_op jit(solution)/shard_map/ppermute | solution.py:31
  129.5 1.7 convert_element_type.95
  131.2 11.4 %all-to-all-done = bf16[16,384,256]{2,1,0:T(8,128)(2,1)S(1)} async-done(((bf16[16,384,256]{2,1,0:T(8,128)(2,1)}), bf16[16,384,256]{2,1,0:T(8,128)(2,1)S(1)}, u32[]{:S(2)}, u32[]{:S(2)}) %all-to-all-start) | async-done | bytes 3145760 | tf_op jit(solution)/shard_map/all_to_all | solution.py:112
  142.6 1.8 gather_fusion.1
  144.4 1.7 broadcast_select_fusion
  146.1 1.1 fusion.31
  148.3 30.5 %all-gather.7.cloned.1.call-done = bf16[16,576,512]{2,1,0:T(8,128)(2,1)} async-done(((bf16[2,576,512]{2,1,0:T(8,128)(2,1)}), bf16[16,576,512]{2,1,0:T(8,128)(2,1)}) %all-gather.7.cloned.1.call-update) | async-done | bytes 9437200 | tf_op jit(solution)/shard_map/all_gather | solution.py:43
  178.7 8.2 %copy.40 = bf16[2,8,1,576,512]{4,3,1,0,2:T(8,128)(2,1)} copy(bf16[2,8,1,576,512]{4,3,0,1,2:T(8,128)(2,1)} %bitcast.70) | data formatting | bytes 18874368 | tf_op jit(solution)/shard_map/transpose | solution.py:47
  186.9 5.7 %multiply_reduce_fusion = f32[576]{0:T(1024)S(1)} fusion(bf16[1,576,16,512]{3,1,2,0:T(8,128)(2,1)} %bitcast.68), kind=kLoop, calls=%fused_computation.5 | loop fusion | flops 14155200 | bytes 9439488 | tf_op jit(solution)/shard_map/reduce_sum | solution.py:91
  193.4 1.3 subtract_convert_fusion.1
  195.7 8.7 %copy.53 = bf16[72,8,16,512]{3,1,2,0:T(8,128)(2,1)} copy(bf16[72,8,16,512]{3,1,0,2:T(8,128)(2,1)} %bitcast.69) | data formatting | bytes 18874368
  204.4 10.7 %convolution_multiply_fusion = f32[576,256]{0,1:T(8,128)S(1)} fusion(bf16[576,8192]{1,0:T(8,128)(2,1)} %bitcast.71, bf16[8192,256]{1,0:T(8,128)(2,1)} %param.8, f32[576]{0:T(1024)S(1)} %add_rsqrt_fusion), kind=kOutput, calls=%fused_computation.21 | convolution fusion | flops 2416066560 | bytes 14223616 | tf_op jit(solution)/shard_map/dot_general | solution.py:90
  215.6 1.6 pad_maximum_fusion.1
  217.2 1.7 copy.42
  218.9 1.7 copy.41
  220.6 5.0 %scatter_fusion.1 = bf16[3072,128]{1,0:T(8,128)(2,1)S(1)} fusion(bf16[3072,128]{1,0:T(8,128)(2,1)S(1)} %pad_maximum_fusion, s32[576]{0:T(1024)S(1)} %fusion.25, bf16[576,128]{1,0:T(8,128)(2,1)} %copy.42), kind=kCustom, calls=%fused_computation.3 | custom fusion | bytes 444672 | tf_op jit(solution)/shard_map/scatter | solution.py:123
  225.6 5.3 %scatter_fusion = bf16[3072,128]{1,0:T(8,128)(2,1)S(1)} fusion(bf16[3072,128]{1,0:T(8,128)(2,1)S(1)} %bitcast.73, s32[576]{0:T(1024)S(1)} %fusion.25, bf16[576,128]{1,0:T(8,128)(2,1)} %copy.41), kind=kCustom, calls=%fused_computation.2 | custom fusion | bytes 444672 | tf_op jit(solution)/shard_map/scatter | solution.py:124
  230.9 1.3 multiply_subtract_fusion
  232.2 12.1 %fusion.33 = (f32[2,576]{1,0:T(2,128)S(1)}, f32[2,576,3072]{2,1,0:T(8,128)}) fusion(pred[576,3072]{1,0:T(8,128)(4,1)} %iota_compare_fusion, bf16[3072,128]{1,0:T(8,128)(2,1)S(1)} %scatter_fusion.1, f32[576,2,64]{2,0,1:T(8,128)} %get-tuple-element.11, f32[576,2,64]{2,0,1:T(8,128)} %get-tuple-element.10), kind=kOutput, calls=%fused_computation.82 | convolution fusion | flops 917031936 | bytes 17306112 | tf_op jit(solution)/shard_map/sub | solution.py:129
  244.2 7.5 %fusion.9 = bf16[576,2,128]{2,0,1:T(8,128)(2,1)S(1)} fusion(f32[2,576,3072]{2,1,0:T(8,128)} %get-tuple-element.25, f32[2,576]{1,0:T(2,128)S(1)} %get-tuple-element.24, bf16[3072,128]{1,0:T(8,128)(2,1)} %copy-done.3, pred[576]{0:T(1024)(128)(4,1)S(1)} %iota_compare_fusion.1), kind=kOutput, calls=%fused_computation.24 | convolution fusion | flops 913342464 | bytes 15242304 | tf_op jit(solution)/shard_map/grs,sd->rgd/dot_general | solution.py:131
  (54 shorter events, 7.5 us)
Async XLA Ops:
  6.5 45.6 %copy-start = (bf16[4,4,384,256]{3,2,1,0:T(8,128)(2,1)S(1)}, bf16[4,4,384,256]{3,2,1,0:T(8,128)(2,1)}, u32[]{:S(2)}) copy-start(bf16[4,4,384,256]{3,2,1,0:T(8,128)(2,1)} %param.10) | copy-start | bytes 9437188
  6.5 32.9 %all-gather.5.cloned.1.call-start = ((), (), s32[]{:S(2)}) async-start(), calls=%async_computation.2 | async-start | bytes 1769472 | tf_op jit(solution)/shard_map/all_gather | solution.py:43
  7.3 171.5 %all-gather.7.cloned.1.call-start = ((), (), s32[]{:S(2)}) async-start(), calls=%async_computation.3 | async-start | bytes 10616832 | tf_op jit(solution)/shard_map/all_gather | solution.py:43
  42.7 9.4 %copy-start.6 = (s32[16,8]{0,1:T(8,128)S(1)}, s32[16,8]{0,1:T(8,128)}, u32[]{:S(2)}) copy-start(s32[16,8]{0,1:T(8,128)} %param.11) | copy-start | bytes 1540
  45.1 45.8 %all-to-all-start.1 = ((bf16[16,576,64]{1,2,0:T(8,128)(2,1)}), bf16[16,576,64]{1,2,0:T(8,128)(2,1)}, u32[]{:S(2)}, u32[]{:S(2)}) async-start(bf16[16,576,64]{1,2,0:T(8,128)(2,1)} %bitcast.72), calls=%async_computation.1 | async-start | bytes 2621440 | tf_op jit(solution)/shard_map/all_to_all | solution.py:26
  57.0 46.0 %copy-start.7 = (s32[1,576]{1,0:T(1,128)S(1)}, s32[1,576]{1,0:T(1,128)}, u32[]{:S(2)}) copy-start(s32[1,576]{1,0:T(1,128)} %param.12) | copy-start | bytes 6916
  90.9 51.7 %all-to-all-start = ((bf16[16,384,256]{2,1,0:T(8,128)(2,1)}), bf16[16,384,256]{2,1,0:T(8,128)(2,1)S(1)}, u32[]{:S(2)}, u32[]{:S(2)}) async-start(bf16[16,384,256]{2,1,0:T(8,128)(2,1)} %select_multiply_fusion), calls=%async_computation | async-start | bytes 6291456 | tf_op jit(solution)/shard_map/all_to_all | solution.py:112
  108.2 9.3 %collective-permute-start = (bf16[576,64]{0,1:T(8,128)(2,1)S(1)}, bf16[576,64]{0,1:T(8,128)(2,1)S(1)}, u32[]{:S(2)}, u32[]{:S(2)}) collective-permute-start(bf16[576,64]{0,1:T(8,128)(2,1)S(1)} %convert_element_type.92), channel_id=1, source_target_pairs={{0,1},{1,0},{2,3},{3,2},{4,5},{5,4},{6,7},{7,6},{8,9},{9,8},{10,11... | collective-permute-start | bytes 221192 | tf_op jit(solution)/shard_map/ppermute | solution.py:31
  118.2 11.3 %collective-permute-start.1 = (bf16[576,128]{0,1:T(8,128)(2,1)}, bf16[576,128]{0,1:T(8,128)(2,1)}, u32[]{:S(2)}, u32[]{:S(2)}) collective-permute-start(bf16[576,128]{0,1:T(8,128)(2,1)} %get-tuple-element.5), channel_id=1, source_target_pairs={{0,2},{1,3},{2,0},{3,1},{4,6},{5,7},{6,4},{7,5},{8,10},{9,11},{10,... | collective-permute-start | bytes 442376 | tf_op jit(solution)/shard_map/ppermute | solution.py:31
  186.9 5.7 %copy-start.4 = (f32[576,128]{0,1:T(8,128)S(1)}, f32[576,128]{0,1:T(8,128)}, u32[]{:S(2)}) copy-start(f32[576,128]{0,1:T(8,128)} %convert_element_type.95) | copy-start | bytes 884740
  215.1 10.5 %copy-start.2 = (bf16[8,384,128]{2,1,0:T(8,128)(2,1)S(1)}, bf16[8,384,128]{2,1,0:T(8,128)(2,1)}, u32[]{:S(2)}) copy-start(bf16[8,384,128]{2,1,0:T(8,128)(2,1)} %get-tuple-element.14) | copy-start | bytes 2359300
  215.6 15.3 %copy-start.5 = (f32[576,64]{1,0:T(8,128)S(1)}, f32[576,64]{1,0:T(8,128)}, u32[]{:S(2)}) copy-start(f32[576,64]{1,0:T(8,128)} %copy.48) | copy-start | bytes 442372
  230.9 13.3 %copy-start.3 = (bf16[3072,128]{1,0:T(8,128)(2,1)}, bf16[3072,128]{1,0:T(8,128)(2,1)S(1)}, u32[]{:S(2)}) copy-start(bf16[3072,128]{1,0:T(8,128)(2,1)S(1)} %scatter_fusion) | copy-start | bytes 2359300
  244.2 8.7 %copy-start.1 = (bf16[4,4,384,256]{3,2,1,0:T(8,128)(2,1)S(1)}, bf16[4,4,384,256]{3,2,1,0:T(8,128)(2,1)}, u32[]{:S(2)}) copy-start(bf16[4,4,384,256]{3,2,1,0:T(8,128)(2,1)} %param.10) | copy-start | bytes 9437188
Sparse Core Ops, SparseCore 0:
  9.1 30.2 all-gather.4
  41.2 137.4 all-gather.6
where the time goes:
time: 260 us
  waiting for transfers between devices  125 us (48%)
  local copies, waits for them, and re-layouts  41.2 us (16%)
  matrix products  33.4 us (13%)
  starting transfers between devices  23.5 us (9%)
  other arithmetic  22.5 us (9%)
  between operations  14.3 us (6%)
    all_gather x2, waiting for transfers between devices, stacked_from(): parts = lax.all_gather(parts, axes[k], axis=0, tiled=True)  62.6 us
    all_to_all x1, waiting for transfers between devices, summed_on_arrival(): lax.all_to_all(parts, axis, split_axis=0, concat_axis=0, tiled=True)  33.9 us
    ppermute x2, waiting for transfers between devices, from_partner(): lax.ppermute(value, axis, [(i, i ^ 1 << bit) for i in range(lax.axis_size...  16.2 us
    all_to_all x1, starting transfers between devices, local(): lax.all_to_all(outgoing, 'store', split_axis=0, concat_axis=0, tiled=True)  12.1 us
    sub x1, matrix products, local(): shifted = jnp.exp(scores - row_max)  12.1 us
    all_to_all x1, waiting for transfers between devices, local(): lax.all_to_all(outgoing, 'store', split_axis=0, concat_axis=0, tiled=True)  11.4 us
    dot_general x1, matrix products, local(): running = jnp.dot(token_part, w_query, preferred_element_type=jnp.float32)  10.7 us
    unnamed x19, local copies, waits for them, and re-layouts  9.17 us
  transfers between devices with their start and end apart: 6, of which 6 were waited for; matrix products, arithmetic and copies ran while one was open for 9% of the time, Pallas kernels for 0%

commit v1 on v0

--- a/solution.py
+++ b/solution.py
@@ -40,7 +40,13 @@
 def stacked_from(value, axes, sequence):
     parts = value[None]
     for k in sequence:
-        parts = lax.all_gather(parts, axes[k], axis=0, tiled=True)
+        try_all_sources_all_all = lambda v0, link_axis: jnp.concatenate(
+            lax.all_to_all(
+                jnp.stack([v0 for _ in range(lax.axis_size(link_axis))]), link_axis, 0, 0
+            ),
+            axis=0,
+        )
+        parts = try_all_sources_all_all(parts, axes[k])
     held = [lax.axis_size(axes[k]) for k in reversed(sequence)]
     parts = parts.reshape(*held, *value.shape)
     turned = sorted(range(len(sequence)), key=lambda place: sequence[len(sequence) - 1 - place])

time: 260 us -> 419 us (1.61)
  waiting for transfers between devices: 125 us -> 237 us
  blocking collectives: 0 us -> 50 us
  between operations: 14.3 us -> 1.05 us
  local copies, waits for them, and re-layouts: 41.2 us -> 48.7 us
    ppermute x2, waiting for transfers between devices: 16.2 us -> 205 us  [from_partner(): lax.ppermute(value, axis, [(i, i ^ 1 << bit) for i in range(lax.axis_size...]
    all_gather x2 -> x0, waiting for transfers between devices: 62.6 us -> none  [stacked_from(): parts = lax.all_gather(parts, axes[k], axis=0, tiled=True)]
    all_to_all x0 -> x1, blocking collectives: none -> 50 us  [local(): lax.all_to_all(outgoing, 'store', split_axis=0, concat_axis=0, tiled=True)]
    all_to_all x1, waiting for transfers between devices: 33.9 us -> 22.6 us  [summed_on_arrival(): lax.all_to_all(parts, axis, split_axis=0, concat_axis=0, tiled=True)]
    all_to_all x0 -> x1, local copies, waits for them, and re-layouts: none -> 8.17 us  [stacked_from(): lax.all_to_all(jnp.stack([v0 for _ in range(lax.axis_size(link_axis))]),...]
    transpose x1 -> x0, local copies, waits for them, and re-layouts: 8.17 us -> none  [stacked_from(): parts.transpose(*turned, *range(len(sequence), parts.ndim))]
    another operation x0 -> x1, local copies, waits for them, and re-layouts: none -> 5.84 us  [stacked_from(): jnp.stack([v0 for _ in range(lax.axis_size(link_axis))])]
    all_to_all x1 -> x2, waiting for transfers between devices: 11.4 us -> 8.86 us  [stacked_from(): lax.all_to_all(jnp.stack([v0 for _ in range(lax.axis_size(link_axis))]),...]
  transfers between devices with their start and end apart: 6 -> 5, of which waited for: 6 -> 4; matrix products, arithmetic and copies ran while one was open for 9% -> 6% of each run, Pallas kernels for 0% -> 0%
where the time goes in v1:
time: 419 us; the launch traced here: 417 us
  waiting for transfers between devices  237 us (57%)
  blocking collectives  50 us (12%)
  local copies, waits for them, and re-layouts  48.7 us (12%)
  matrix products  33.4 us (8%)
  other arithmetic  25.4 us (6%)
  starting transfers between devices  21 us (5%)
    ppermute x2, waiting for transfers between devices, from_partner(): lax.ppermute(value, axis, [(i, i ^ 1 << bit) for i in range(lax.axis_size...  205 us
    all_to_all x1, blocking collectives, local(): lax.all_to_all(outgoing, 'store', split_axis=0, concat_axis=0, tiled=True)  50 us
    all_to_all x1, waiting for transfers between devices, summed_on_arrival(): lax.all_to_all(parts, axis, split_axis=0, concat_axis=0, tiled=True)  22.6 us
    sub x1, matrix products, local(): shifted = jnp.exp(scores - row_max)  12.1 us
    dot_general x1, matrix products, local(): running = jnp.dot(token_part, w_query, preferred_element_type=jnp.float32)  10.7 us
    all_to_all x2, starting transfers between devices, stacked_from(): lax.all_to_all(jnp.stack([v0 for _ in range(lax.axis_size(link_axis))]),...  9.92 us
    unnamed x21, local copies, waits for them, and re-layouts  9.17 us
    all_to_all x2, waiting for transfers between devices, stacked_from(): lax.all_to_all(jnp.stack([v0 for _ in range(lax.axis_size(link_axis))]),...  8.86 us
  transfers between devices with their start and end apart: 5, of which 4 were waited for; matrix products, arithmetic and copies ran while one was open for 6% of the time, Pallas kernels for 0%

profile of v1, /device:TPU:33, one launch (start us, length us, event | category | flops | bytes accessed | tf_op | source)
XLA Modules:
  0.0 416.5 jit_solution(3603044836555482971)
XLA Ops:
  0.0 2.5 pad_maximum_fusion
  2.5 4.5 %all-to-all-start.2 = ((bf16[2,1,1,576,512]{4,3,2,1,0:T(8,128)(2,1)}), bf16[2,1,1,576,512]{4,3,2,1,0:T(8,128)(2,1)}, u32[]{:S(2)}, u32[]{:S(2)}) async-start(bf16[2,1,1,576,512]{4,3,2,1,0:T(8,128)(2,1)} %pad_maximum_fusion), calls=%async_computation.2 | async-start | bytes 2359296 | tf_op jit(solution)/shard_map/all_to_all | solution.py:44
  7.0 3.2 convolution_convert_fusion
  10.2 2.4 copy.33
  12.7 8.9 %all-to-all-done.2 = bf16[2,1,1,576,512]{4,3,2,1,0:T(8,128)(2,1)} async-done(((bf16[2,1,1,576,512]{4,3,2,1,0:T(8,128)(2,1)}), bf16[2,1,1,576,512]{4,3,2,1,0:T(8,128)(2,1)}, u32[]{:S(2)}, u32[]{:S(2)}) %all-to-all-start.2) | async-done | bytes 1179680 | tf_op jit(solution)/shard_map/all_to_all | solution.py:44
  21.5 8.0 %all-to-all-start.1 = ((bf16[16,576,64]{1,2,0:T(8,128)(2,1)}), bf16[16,576,64]{1,2,0:T(8,128)(2,1)}, u32[]{:S(2)}, u32[]{:S(2)}) async-start(bf16[16,576,64]{1,2,0:T(8,128)(2,1)} %bitcast.72), calls=%async_computation.1 | async-start | bytes 2621440 | tf_op jit(solution)/shard_map/all_to_all | solution.py:26
  30.6 3.5 gather_fusion
  34.2 2.3 select_multiply_fusion
  36.4 22.6 %all-to-all-done.1 = bf16[16,576,64]{1,2,0:T(8,128)(2,1)} async-done(((bf16[16,576,64]{1,2,0:T(8,128)(2,1)}), bf16[16,576,64]{1,2,0:T(8,128)(2,1)}, u32[]{:S(2)}, u32[]{:S(2)}) %all-to-all-start.1) | async-done | bytes 1179680 | tf_op jit(solution)/shard_map/all_to_all | solution.py:26
  59.0 50.0 %all_to_all.20 = bf16[16,384,256]{2,1,0:T(8,128)(2,1)} all-to-all(bf16[16,384,256]{2,1,0:T(8,128)(2,1)S(1)} %select_multiply_fusion), channel_id=1, replica_groups=mesh['store'=16,'tp_0'=2,'tp_1'=8] {'store'}, dimensions={0} | all-to-all | bytes 6291456 | tf_op jit(solution)/shard_map/all_to_all | solution.py:118
  109.0 5.8 %stack.7 = bf16[8,2,1,576,512]{4,3,1,2,0:T(8,128)(2,1)} broadcast(bf16[2,576,512]{2,1,0:T(8,128)(2,1)} %bitcast.11), dimensions={1,3,4} | broadcast | bytes 10616832 | tf_op jit(solution)/shard_map/stack | solution.py:45
  114.8 5.4 %all-to-all-start.3 = ((bf16[8,2,1,576,512]{4,3,1,2,0:T(8,128)(2,1)}), bf16[8,2,1,576,512]{4,3,1,2,0:T(8,128)(2,1)}, u32[]{:S(2)}, u32[]{:S(2)}) async-start(bf16[8,2,1,576,512]{4,3,1,2,0:T(8,128)(2,1)} %stack.7), calls=%async_computation.3 | async-start | bytes 18874368 | tf_op jit(solution)/shard_map/all_to_all | solution.py:44
  121.4 2.6 iota_compare_fusion
  124.1 1.5 convert_reduce_fusion
  125.9 199.5 %collective-permute-done = bf16[576,64]{0,1:T(8,128)(2,1)S(1)} collective-permute-done((bf16[576,64]{0,1:T(8,128)(2,1)S(1)}, bf16[576,64]{0,1:T(8,128)(2,1)S(1)}, u32[]{:S(2)}, u32[]{:S(2)}) %collective-permute-start) | collective-permute-done | bytes 73760 | tf_op jit(solution)/shard_map/ppermute | solution.py:31
  326.0 2.8 collective-permute-start.1
  328.9 6.0 %collective-permute-done.1 = bf16[576,128]{0,1:T(8,128)(2,1)} collective-permute-done((bf16[576,128]{0,1:T(8,128)(2,1)}, bf16[576,128]{0,1:T(8,128)(2,1)}, u32[]{:S(2)}, u32[]{:S(2)}) %collective-permute-start.1) | collective-permute-done | bytes 147488 | tf_op jit(solution)/shard_map/ppermute | solution.py:31
  334.9 1.7 convert_element_type.95
  336.6 1.8 gather_fusion.1
  338.4 1.6 broadcast_select_fusion
  342.3 8.2 %copy.34 = bf16[8,2,1,576,512]{4,3,0,1,2:T(8,128)(2,1)} copy(bf16[8,2,1,576,512]{4,3,1,2,0:T(8,128)(2,1)} %all-to-all-done.3) | data formatting | bytes 18874368 | tf_op jit(solution)/shard_map/all_to_all | solution.py:44
  350.5 5.7 %multiply_reduce_fusion = f32[576]{0:T(1024)S(1)} fusion(bf16[1,576,16,512]{3,1,2,0:T(8,128)(2,1)} %bitcast.69), kind=kLoop, calls=%fused_computation.5 | loop fusion | flops 14155200 | bytes 9439488 | tf_op jit(solution)/shard_map/reduce_sum | solution.py:97
  356.9 1.3 subtract_convert_fusion.1
  359.2 8.7 %copy.47 = bf16[72,8,16,512]{3,1,2,0:T(8,128)(2,1)} copy(bf16[72,8,16,512]{3,1,0,2:T(8,128)(2,1)} %bitcast.70) | data formatting | bytes 18874368
  367.9 10.7 %convolution_multiply_fusion = f32[576,256]{0,1:T(8,128)S(1)} fusion(bf16[576,8192]{1,0:T(8,128)(2,1)} %bitcast.71, bf16[8192,256]{1,0:T(8,128)(2,1)} %param.8, f32[576]{0:T(1024)S(1)} %add_rsqrt_fusion), kind=kOutput, calls=%fused_computation.21 | convolution fusion | flops 2416066560 | bytes 14223616 | tf_op jit(solution)/shard_map/dot_general | solution.py:96
  379.1 1.6 pad_maximum_fusion.2
  380.7 1.7 copy.36
  382.4 1.7 copy.35
  384.1 5.0 %scatter_fusion.1 = bf16[3072,128]{1,0:T(8,128)(2,1)S(1)} fusion(bf16[3072,128]{1,0:T(8,128)(2,1)S(1)} %pad_maximum_fusion.1, s32[576]{0:T(1024)S(1)} %fusion.25, bf16[576,128]{1,0:T(8,128)(2,1)} %copy.36), kind=kCustom, calls=%fused_computation.3 | custom fusion | bytes 444672 | tf_op jit(solution)/shard_map/scatter | solution.py:129
  389.2 5.3 %scatter_fusion = bf16[3072,128]{1,0:T(8,128)(2,1)S(1)} fusion(bf16[3072,128]{1,0:T(8,128)(2,1)S(1)} %bitcast.73, s32[576]{0:T(1024)S(1)} %fusion.25, bf16[576,128]{1,0:T(8,128)(2,1)} %copy.35), kind=kCustom, calls=%fused_computation.2 | custom fusion | bytes 444672 | tf_op jit(solution)/shard_map/scatter | solution.py:130
  395.7 12.1 %fusion.33 = (f32[2,576]{1,0:T(2,128)S(1)}, f32[2,576,3072]{2,1,0:T(8,128)}) fusion(pred[576,3072]{1,0:T(8,128)(4,1)} %iota_compare_fusion, bf16[3072,128]{1,0:T(8,128)(2,1)S(1)} %scatter_fusion.1, f32[576,2,64]{2,0,1:T(8,128)} %get-tuple-element.11, f32[576,2,64]{2,0,1:T(8,128)} %get-tuple-element.10), kind=kOutput, calls=%fused_computation.83 | convolution fusion | flops 917031936 | bytes 17306112 | tf_op jit(solution)/shard_map/sub | solution.py:135
  407.8 7.5 %fusion.9 = bf16[576,2,128]{2,0,1:T(8,128)(2,1)S(1)} fusion(f32[2,576,3072]{2,1,0:T(8,128)} %get-tuple-element.25, f32[2,576]{1,0:T(2,128)S(1)} %get-tuple-element.24, bf16[3072,128]{1,0:T(8,128)(2,1)} %copy-done.4, pred[576]{0:T(1024)(128)(4,1)S(1)} %iota_compare_fusion.1), kind=kOutput, calls=%fused_computation.25 | convolution fusion | flops 913342464 | bytes 15242304 | tf_op jit(solution)/shard_map/grs,sd->rgd/dot_general | solution.py:137
  (55 shorter events, 9.4 us)
Async XLA Ops:
  0.0 29.6 %copy-start = (bf16[4,4,384,256]{3,2,1,0:T(8,128)(2,1)S(1)}, bf16[4,4,384,256]{3,2,1,0:T(8,128)(2,1)}, u32[]{:S(2)}) copy-start(bf16[4,4,384,256]{3,2,1,0:T(8,128)(2,1)} %param.10) | copy-start | bytes 9437188
  2.5 19.0 %all-to-all-start.2 = ((bf16[2,1,1,576,512]{4,3,2,1,0:T(8,128)(2,1)}), bf16[2,1,1,576,512]{4,3,2,1,0:T(8,128)(2,1)}, u32[]{:S(2)}, u32[]{:S(2)}) async-start(bf16[2,1,1,576,512]{4,3,2,1,0:T(8,128)(2,1)} %pad_maximum_fusion), calls=%async_computation.2 | async-start | bytes 2359296 | tf_op jit(solution)/shard_map/all_to_all | solution.py:44
  10.2 19.3 %copy-start.7 = (s32[16,8]{0,1:T(8,128)S(1)}, s32[16,8]{0,1:T(8,128)}, u32[]{:S(2)}) copy-start(s32[16,8]{0,1:T(8,128)} %param.11) | copy-start | bytes 1540
  21.5 37.5 %all-to-all-start.1 = ((bf16[16,576,64]{1,2,0:T(8,128)(2,1)}), bf16[16,576,64]{1,2,0:T(8,128)(2,1)}, u32[]{:S(2)}, u32[]{:S(2)}) async-start(bf16[16,576,64]{1,2,0:T(8,128)(2,1)} %bitcast.72), calls=%async_computation.1 | async-start | bytes 2621440 | tf_op jit(solution)/shard_map/all_to_all | solution.py:26
  114.8 5.4 %copy-start.8 = (s32[1,576]{1,0:T(1,128)S(1)}, s32[1,576]{1,0:T(1,128)}, u32[]{:S(2)}) copy-start(s32[1,576]{1,0:T(1,128)} %param.12) | copy-start | bytes 6916
  114.8 227.5 %all-to-all-start.3 = ((bf16[8,2,1,576,512]{4,3,1,2,0:T(8,128)(2,1)}), bf16[8,2,1,576,512]{4,3,1,2,0:T(8,128)(2,1)}, u32[]{:S(2)}, u32[]{:S(2)}) async-start(bf16[8,2,1,576,512]{4,3,1,2,0:T(8,128)(2,1)} %stack.7), calls=%async_computation.3 | async-start | bytes 18874368 | tf_op jit(solution)/shard_map/all_to_all | solution.py:44
  120.3 216.3 %copy-start.2 = (bf16[16,384,256]{2,1,0:T(8,128)(2,1)S(1)}, bf16[16,384,256]{2,1,0:T(8,128)(2,1)}, u32[]{:S(2)}) copy-start(bf16[16,384,256]{2,1,0:T(8,128)(2,1)} %all_to_all.20) | copy-start | bytes 9437188
  125.6 199.7 %collective-permute-start = (bf16[576,64]{0,1:T(8,128)(2,1)S(1)}, bf16[576,64]{0,1:T(8,128)(2,1)S(1)}, u32[]{:S(2)}, u32[]{:S(2)}) collective-permute-start(bf16[576,64]{0,1:T(8,128)(2,1)S(1)} %convert_element_type.92), channel_id=1, source_target_pairs={{0,1},{1,0},{2,3},{3,2},{4,5},{5,4},{6,7},{7,6},{8,9},{9,8},{10,11... | collective-permute-start | bytes 221192 | tf_op jit(solution)/shard_map/ppermute | solution.py:31
  326.0 8.9 %collective-permute-start.1 = (bf16[576,128]{0,1:T(8,128)(2,1)}, bf16[576,128]{0,1:T(8,128)(2,1)}, u32[]{:S(2)}, u32[]{:S(2)}) collective-permute-start(bf16[576,128]{0,1:T(8,128)(2,1)} %get-tuple-element.5), channel_id=1, source_target_pairs={{0,2},{1,3},{2,0},{3,1},{4,6},{5,7},{6,4},{7,5},{8,10},{9,11},{10,... | collective-permute-start | bytes 442376 | tf_op jit(solution)/shard_map/ppermute | solution.py:31
  350.5 5.7 %copy-start.5 = (f32[576,128]{0,1:T(8,128)S(1)}, f32[576,128]{0,1:T(8,128)}, u32[]{:S(2)}) copy-start(f32[576,128]{0,1:T(8,128)} %convert_element_type.95) | copy-start | bytes 884740
  378.6 10.6 %copy-start.3 = (bf16[8,384,128]{2,1,0:T(8,128)(2,1)S(1)}, bf16[8,384,128]{2,1,0:T(8,128)(2,1)}, u32[]{:S(2)}) copy-start(bf16[8,384,128]{2,1,0:T(8,128)(2,1)} %get-tuple-element.14) | copy-start | bytes 2359300
  379.1 15.4 %copy-start.6 = (f32[576,64]{1,0:T(8,128)S(1)}, f32[576,64]{1,0:T(8,128)}, u32[]{:S(2)}) copy-start(f32[576,64]{1,0:T(8,128)} %copy.42) | copy-start | bytes 442372
  394.5 13.3 %copy-start.4 = (bf16[3072,128]{1,0:T(8,128)(2,1)}, bf16[3072,128]{1,0:T(8,128)(2,1)S(1)}, u32[]{:S(2)}) copy-start(bf16[3072,128]{1,0:T(8,128)(2,1)S(1)} %scatter_fusion) | copy-start | bytes 2359300
  407.8 8.7 %copy-start.1 = (bf16[4,4,384,256]{3,2,1,0:T(8,128)(2,1)S(1)}, bf16[4,4,384,256]{3,2,1,0:T(8,128)(2,1)}, u32[]{:S(2)}) copy-start(bf16[4,4,384,256]{3,2,1,0:T(8,128)(2,1)} %param.10) | copy-start | bytes 9437188
